TPU v7x, 32 devices: a whole 2x2x4 slice. The times are simulated.
32 devices in a mesh: row: 4 (over y, x), col: 8 (over z, core).
Axes of the slice: x: 2, y: 2, z: 4, core: 2. Of those that a mesh axis runs over, the one named last changes fastest.
Arguments:
- vorticity: float32 [3, 128, 128, 128], P(None, 'row', 'col'), may hold values from -18.1 to 18.1
- scalar: float32 [256, 256, 256], P('row', 'col'), may hold values from -6 to 6
Outputs:
- advected: float32 [256, 256, 256], P('row', 'col')
All inputs are finite; a program needn't handle non-finite values. Where the computation divides by a largest or mean magnitude, that divisor is 1e-20 or more.
Results may differ from a plain program's by a relative error of at most 0.0003.
Values sent between devices are 32-bit elements; how exact they have to be, the bound alone decides.
A program may use at most 128 MiB of HBM per device.

v0:
```python
import math
import jax
import jax.numpy as jnp
from jax import lax
from jax.sharding import PartitionSpec as P

COURANT = 0.9
EPSILON = 1e-06
HIGHEST = lax.Precision.HIGHEST


def with_halo(cells, sides, width):
    for axis, dim in sides:
        count = lax.axis_size(axis)
        head = lax.slice_in_dim(cells, 0, width, axis=dim)
        tail = lax.slice_in_dim(cells, cells.shape[dim] - width, cells.shape[dim], axis=dim)
        cells = jnp.concatenate(
            [
                lax.ppermute(tail, axis, [(i, (i + 1) % count) for i in range(count)]),
                cells,
                lax.ppermute(head, axis, [((i + 1) % count, i) for i in range(count)]),
            ],
            axis=dim,
        )
    return cells


def kernel_weight(distance):
    radius = jnp.abs(distance)
    inner_lobe = (
        -(radius - 1.0)
        * ((((25.0 * radius - 38.0) * radius - 3.0) * radius + 12.0) * radius + 12.0)
        / 12.0
    )
    middle_lobe = (
        (radius - 1.0)
        * (radius - 2.0)
        * (((25.0 * radius - 114.0) * radius + 153.0) * radius - 48.0)
        / 24.0
    )
    outer_cube = (radius - 3.0) * (radius - 3.0) * (radius - 3.0)
    outer_lobe = -(radius - 2.0) * outer_cube * (5.0 * radius - 8.0) / 24.0
    return jnp.where(
        radius < 1.0,
        inner_lobe,
        jnp.where(radius < 2.0, middle_lobe, jnp.where(radius < 3.0, outer_lobe, 0.0)),
    )


def tables(length):
    indices = jnp.arange(length, dtype=jnp.int32)
    product = indices[:, None] * indices[None, :] % length
    angle = product.astype(jnp.float32) * (2.0 * math.pi / length)
    return (jnp.cos(angle), jnp.sin(angle))


def rotate(complex_pair, formula, cosine, sine, direction):
    real_cos = jnp.einsum(formula, complex_pair[0], cosine, precision=HIGHEST)
    real_sin = jnp.einsum(formula, complex_pair[0], sine, precision=HIGHEST)
    imag_cos = jnp.einsum(formula, complex_pair[1], cosine, precision=HIGHEST)
    imag_sin = jnp.einsum(formula, complex_pair[1], sine, precision=HIGHEST)
    return jnp.stack([real_cos - direction * imag_sin, imag_cos + direction * real_sin])


def wavenumber(start, count, length):
    indices = start + jnp.arange(count, dtype=jnp.int32)
    waves = jnp.where(indices < length // 2, indices, indices - length).astype(jnp.float32)
    return (waves, indices == length // 2)


def induce(spectrum, xwaves, ywaves, zwaves, banned, inverse_cube):
    wave_sq = xwaves * xwaves + ywaves * ywaves + zwaves * zwaves
    keep = (wave_sq > 0.0) & jnp.logical_not(banned)
    factor = jnp.where(keep, 1.0 / jnp.maximum(wave_sq, 1.0), 0.0) * inverse_cube
    crosses = []
    for part_index in range(2):
        omega = spectrum[part_index]
        crosses.append(
            jnp.stack(
                [
                    ywaves * omega[2] - zwaves * omega[1],
                    zwaves * omega[0] - xwaves * omega[2],
                    xwaves * omega[1] - ywaves * omega[0],
                ]
            )
        )
    return jnp.stack([-crosses[1] * factor, crosses[0] * factor])


def merged_shape(lower, grid_axis):
    shape = list(lower.shape)
    shape[grid_axis] = 2 * shape[grid_axis]
    return shape


def refine_roll(coarse, grid_axis):
    lower = 0.75 * coarse + 0.25 * jnp.roll(coarse, 1, grid_axis)
    upper = 0.75 * coarse + 0.25 * jnp.roll(coarse, -1, grid_axis)
    return jnp.stack([lower, upper], axis=grid_axis + 1).reshape(merged_shape(lower, grid_axis))


def refine_rim(coarse, grid_axis):
    length = coarse.shape[grid_axis]
    inner = lax.slice_in_dim(coarse, 1, length - 1, axis=grid_axis)
    below = lax.slice_in_dim(coarse, 0, length - 2, axis=grid_axis)
    above = lax.slice_in_dim(coarse, 2, length, axis=grid_axis)
    lower = 0.75 * inner + 0.25 * below
    upper = 0.75 * inner + 0.25 * above
    return jnp.stack([lower, upper], axis=grid_axis + 1).reshape(merged_shape(lower, grid_axis))


def remesh_roll(field, displace, grid_axis):
    summed = jnp.zeros(field.shape, jnp.float32)
    for offset in range(-3, 4):
        summed = summed + jnp.roll(field, offset, grid_axis) * kernel_weight(
            offset - jnp.roll(displace, offset, grid_axis)
        )
    return summed


def remesh_rim(field_ext, displace_ext, grid_axis, count):
    shape = list(field_ext.shape)
    shape[grid_axis] = count
    summed = jnp.zeros(shape, jnp.float32)
    for offset in range(-3, 4):
        begin = 3 - offset
        values = lax.slice_in_dim(field_ext, begin, begin + count, axis=grid_axis)
        moved = lax.slice_in_dim(displace_ext, begin, begin + count, axis=grid_axis)
        summed = summed + values * kernel_weight(offset - moved)
    return summed


def shards(vorticity, scalar):
    coarse_n = vorticity.shape[3]
    cos_full, sin_full = tables(coarse_n)
    mode_count = coarse_n // 2
    weights = jnp.where(jnp.arange(mode_count) == 0, 1.0, 2.0).astype(jnp.float32)
    cos_fwd = cos_full[:, :mode_count]
    sin_fwd = sin_full[:, :mode_count]
    cos_back = cos_full[:mode_count, :] * weights[:, None]
    sin_back = sin_full[:mode_count, :] * weights[:, None]
    forward = jnp.stack(
        [
            jnp.einsum("cyzx,xk->cyzk", vorticity, cos_fwd, precision=HIGHEST),
            -jnp.einsum("cyzx,xk->cyzk", vorticity, sin_fwd, precision=HIGHEST),
        ]
    )
    spectrum = rotate(
        lax.all_to_all(forward, "row", split_axis=4, concat_axis=2, tiled=True),
        "cyzk,yq->czkq",
        cos_full,
        sin_full,
        -1.0,
    )
    spectrum = rotate(
        lax.all_to_all(spectrum, "col", split_axis=4, concat_axis=2, tiled=True),
        "czkq,zw->ckqw",
        cos_full,
        sin_full,
        -1.0,
    )
    first_count = spectrum.shape[2]
    second_count = spectrum.shape[3]
    xwaves, xnyquist = wavenumber(lax.axis_index("row") * first_count, first_count, coarse_n)
    ywaves, ynyquist = wavenumber(lax.axis_index("col") * second_count, second_count, coarse_n)
    zwaves, znyquist = wavenumber(0, coarse_n, coarse_n)
    banned = xnyquist[:, None, None] | ynyquist[None, :, None] | znyquist[None, None, :]
    inverse_cube = 1.0 / (coarse_n * coarse_n * coarse_n)
    velocity_hat = induce(
        spectrum,
        xwaves[:, None, None],
        ywaves[None, :, None],
        zwaves[None, None, :],
        banned,
        inverse_cube,
    )
    inverse_z = rotate(velocity_hat, "ckqw,wz->ckqz", cos_full, sin_full, 1.0)
    mixed = rotate(
        lax.all_to_all(inverse_z, "col", split_axis=4, concat_axis=3, tiled=True),
        "ckqz,qy->ckzy",
        cos_full,
        sin_full,
        1.0,
    )
    block = lax.all_to_all(mixed, "row", split_axis=4, concat_axis=2, tiled=True)
    velocity = jnp.einsum("ckzy,kx->cyzx", block[0], cos_back, precision=HIGHEST) - jnp.einsum(
        "ckzy,kx->cyzx", block[1], sin_back, precision=HIGHEST
    )
    velocity_peak = lax.pmax(jnp.max(jnp.abs(velocity)), ("row", "col"))
    courant_scale = COURANT / (velocity_peak + EPSILON)
    fine_rows = scalar.shape[0]
    fine_cols = scalar.shape[1]
    rimmed = with_halo(velocity, (("row", 1), ("col", 2)), 1)
    displaced = refine_rim(refine_rim(refine_roll(rimmed, 3), 1), 2) * courant_scale
    swept = remesh_roll(scalar, displaced[0], 2)
    rows_input = jnp.stack([swept, displaced[1]])
    rows_ext = with_halo(rows_input, (("row", 1),), 3)
    ymoved = rows_ext[1]
    swept = remesh_rim(rows_ext[0], ymoved, 0, fine_rows)
    cols_input = jnp.stack([swept, displaced[2]])
    cols_ext = with_halo(cols_input, (("col", 2),), 3)
    zmoved = cols_ext[1]
    return remesh_rim(cols_ext[0], zmoved, 1, fine_cols)


def solution(mesh):
    in_specs = (P(None, "row", "col", None), P("row", "col", None))
    out_specs = P("row", "col", None)
    return jax.shard_map(shards, mesh=mesh, in_specs=in_specs, out_specs=out_specs, check_vma=False)
```

profile of v0, /device:TPU:1, one launch (start us, length us, event | category | flops | bytes accessed | tf_op | source)
XLA Modules:
  0.0 478.1 jit_solution(8644423327381944516)
XLA Ops:
  3.1 2.5 copy.292
  5.6 3.4 reshape.296
  9.0 14.5 %all_to_all.60 = f32[4,1,49152]{2,1,0:T(1,128)S(1)} all-to-all(f32[4,1,49152]{2,1,0:T(1,128)S(1)} %reshape.296), channel_id=1, replica_groups=mesh['row'=4,'col'=8] {'row'}, dimensions={0} | all-to-all | bytes 1572864 | tf_op jit(solution)/shard_map/all_to_all | solution.py:149
  24.0 3.0 reduce
  27.0 2.7 reshape.297
  29.7 3.7 copy.293
  35.6 2.1 squeeze.23
  40.3 2.1 squeeze.22
  44.6 6.5 %copy.296 = f32[2,3,16,16,128]{3,2,1,0,4:T(8,128)} copy(f32[2,3,16,16,128]{4,3,2,1,0:T(8,128)S(1)} %pad_maximum_fusion.7) | data formatting | bytes 1572864 | tf_op jit(solution)/shard_map/stack | solution.py:62
  51.2 5.5 %reshape.298 = f32[8,1,24576]{2,1,0:T(1,128)} reshape(f32[128,2,3,16,16]{4,3,2,1,0:T(8,128)} %bitcast.181) | data formatting | bytes 1572864
  56.6 7.0 %all-to-all-start.1 = ((f32[8,1,24576]{2,1,0:T(1,128)}), f32[8,1,24576]{2,1,0:T(1,128)S(1)}, u32[]{:S(2)}, u32[]{:S(2)}) async-start(f32[8,1,24576]{2,1,0:T(1,128)} %reshape.298), calls=%async_computation.1 | async-start | bytes 1572864 | tf_op jit(solution)/shard_map/all_to_all | solution.py:156
  64.0 19.6 %all-to-all-done.1 = f32[8,1,24576]{2,1,0:T(1,128)S(1)} async-done(((f32[8,1,24576]{2,1,0:T(1,128)}), f32[8,1,24576]{2,1,0:T(1,128)S(1)}, u32[]{:S(2)}, u32[]{:S(2)}) %all-to-all-start.1) | async-done | bytes 786464 | tf_op jit(solution)/shard_map/all_to_all | solution.py:156
  83.7 2.6 reduce.1
  86.2 4.8 reshape.299
  91.0 8.0 %copy.297 = f32[2,3,16,16,8,16]{2,4,5,3,1,0:T(8,128)} copy(f32[2,3,16,16,8,16]{3,2,1,0,5,4:T(8,128)} %bitcast.182) | data formatting | bytes 1572864 | tf_op jit(solution)/shard_map/all_to_all | solution.py:156
  99.0 6.3 %fusion.342 = (f32[1,3,8,16,16,16]{3,2,5,4,1,0:T(8,128)}, f32[1,3,8,16,16,16]{3,2,5,4,1,0:T(8,128)}) fusion(f32[2,3,8,16,16,16]{3,2,5,4,1,0:T(8,128)} %bitcast.179), kind=kLoop, calls=%fused_computation.442 | loop fusion | bytes 1572864 | tf_op jit(solution)/shard_map/slice | solution.py:59
  105.4 2.4 squeeze.25
  108.5 2.6 squeeze.24
  116.4 6.0 %copy.298 = f32[2,3,16,16,128]{3,2,1,0,4:T(8,128)} copy(f32[2,3,16,16,128]{4,3,2,1,0:T(8,128)S(1)} %pad_maximum_fusion.8) | data formatting | bytes 1572864 | tf_op jit(solution)/shard_map/stack | solution.py:62
  122.4 5.6 %reshape.300 = f32[8,1,24576]{2,1,0:T(1,128)} reshape(f32[128,2,3,16,16]{4,3,2,1,0:T(8,128)} %bitcast.183) | data formatting | bytes 1572864
  128.0 5.3 %all-to-all-start.2 = ((f32[8,1,24576]{2,1,0:T(1,128)}), f32[8,1,24576]{2,1,0:T(1,128)}, u32[]{:S(2)}, u32[]{:S(2)}) async-start(f32[8,1,24576]{2,1,0:T(1,128)} %reshape.300), calls=%async_computation.2 | async-start | bytes 1572864 | tf_op jit(solution)/shard_map/all_to_all | solution.py:179
  133.4 2.9 fusion.352
  136.2 2.9 fusion.354
  139.1 14.3 %all-to-all-done.2 = f32[8,1,24576]{2,1,0:T(1,128)} async-done(((f32[8,1,24576]{2,1,0:T(1,128)}), f32[8,1,24576]{2,1,0:T(1,128)}, u32[]{:S(2)}, u32[]{:S(2)}) %all-to-all-start.2) | async-done | bytes 786464 | tf_op jit(solution)/shard_map/all_to_all | solution.py:179
  153.4 3.7 reduce.2
  157.1 4.8 reshape.301
  161.9 6.4 %copy.353 = f32[2,3,16,16,8,16]{3,4,5,2,1,0:T(8,128)S(1)} copy(f32[2,3,16,16,8,16]{3,2,1,0,5,4:T(8,128)} %bitcast.184) | data formatting | bytes 1572864 | tf_op jit(solution)/shard_map/all_to_all | solution.py:179
  168.3 3.1 fusion.341
  171.4 2.4 squeeze.26
  174.6 2.9 squeeze.27
  179.7 6.0 %copy.300 = f32[2,3,16,16,128]{3,2,1,0,4:T(8,128)} copy(f32[2,3,16,16,128]{4,3,2,1,0:T(8,128)S(1)} %pad_maximum_fusion.9) | data formatting | bytes 1572864 | tf_op jit(solution)/shard_map/stack | solution.py:62
  185.7 5.5 %reshape.302 = f32[4,1,49152]{2,1,0:T(1,128)} reshape(f32[128,2,3,16,16]{4,3,2,1,0:T(8,128)} %bitcast.185) | data formatting | bytes 1572864
  191.2 4.2 all-to-all-start.3
  197.1 2.8 fusion.356
  199.9 5.9 %all-to-all-done.3 = f32[4,1,49152]{2,1,0:T(1,128)} async-done(((f32[4,1,49152]{2,1,0:T(1,128)}), f32[4,1,49152]{2,1,0:T(1,128)}, u32[]{:S(2)}, u32[]{:S(2)}) %all-to-all-start.3) | async-done | bytes 786464 | tf_op jit(solution)/shard_map/all_to_all | solution.py:185
  205.8 3.9 reduce.3
  209.6 4.9 %reshape.303 = f32[128,2,3,16,16]{4,3,2,1,0:T(8,128)} reshape(f32[4,49152]{1,0:T(4,128)S(1)} %reduce.3) | data formatting | bytes 1572864
  214.5 6.7 %copy.301 = f32[2,3,16,16,4,32]{5,3,2,4,1,0:T(8,128)} copy(f32[2,3,16,16,4,32]{3,2,1,0,5,4:T(8,128)} %bitcast.186) | data formatting | bytes 1572864 | tf_op jit(solution)/shard_map/all_to_all | solution.py:185
  221.2 3.8 fusion.343
  225.0 2.9 copy.303
  227.9 2.0 copy.302
  242.0 2.6 copy.342
  244.6 2.5 copy.344
  247.2 2.5 copy.346
  249.7 2.6 copy.347
  252.2 2.5 copy.349
  254.8 2.5 copy.351
  267.1 40.1 %pmax.7 = f32[]{:T(128)} all-reduce(f32[]{:T(128)} %get-tuple-element.5), channel_id=1, replica_groups=mesh['row'=4,'col'=8] {'row','col'}, use_global_device_ids=true, to_apply=%region_1.2 | all-reduce | flops 1 | bytes 8 | tf_op jit(solution)/shard_map/pmax | solution.py:189
  312.0 9.8 %copy.310 = f32[3,34,18,128,2]{1,4,3,2,0:T(2,128)} copy(f32[3,34,18,128,2]{3,1,2,0,4:T(8,128)} %pad_maximum_fusion.3) | data formatting | bytes 3760128 | tf_op jit(solution)/shard_map/stack | solution.py:99
  321.8 12.1 %fusion.3 = (f32[3,32,1,18,256]{1,4,3,0,2:T(8,128)}, f32[3,32,1,18,256]{1,4,3,0,2:T(8,128)}) fusion(f32[3,34,18,256]{1,3,2,0:T(8,128)} %bitcast.175), kind=kLoop, calls=%fused_computation.6 | loop fusion | flops 2211840 | bytes 8847360 | tf_op jit(solution)/shard_map/stack | solution.py:109
  333.9 12.6 %pad_maximum_fusion = f32[3,32,2,18,256]{1,4,3,0,2:T(8,128)} fusion(f32[3,32,1,18,256]{1,4,3,0,2:T(8,128)} %get-tuple-element.8, f32[3,32,1,18,256]{1,4,3,0,2:T(8,128)} %get-tuple-element.7), kind=kLoop, calls=%fused_computation | loop fusion | flops 884736 | bytes 7077888 | tf_op jit(solution)/shard_map/stack | solution.py:109
  346.5 11.0 %copy.311 = f32[3,32,2,18,256]{4,2,1,3,0:T(2,128)} copy(f32[3,32,2,18,256]{1,4,3,0,2:T(8,128)} %pad_maximum_fusion) | data formatting | bytes 7077888 | tf_op jit(solution)/shard_map/stack | solution.py:109
  357.5 5.8 %reshape.287 = f32[3,64,18,256]{3,1,2,0:T(8,128)} reshape(f32[3,32,2,18,256]{4,2,1,3,0:T(2,128)} %copy.311) | data formatting | bytes 7077888 | tf_op jit(solution)/shard_map/reshape | solution.py:109
  363.3 4.8 %fusion.7 = (f32[3,64,16,1,256]{4,1,2,0,3:T(8,128)S(1)}, f32[3,64,16,1,256]{4,1,2,0,3:T(8,128)S(1)}) fusion(f32[3,64,18,256]{3,1,2,0:T(8,128)} %reshape.287), kind=kLoop, calls=%fused_computation.18 | loop fusion | flops 3932160 | bytes 15728640 | tf_op jit(solution)/shard_map/stack | solution.py:109
  380.5 23.9 %fusion.21 = f32[1,64,32,256]{3,1,2,0:T(8,128)S(1)} fusion(f32[64,32,3]{2,0,1:T(8,128)S(1)} %copy-done.15, f32[64,32,253]{2,0,1:T(8,128)S(1)} %copy-done.9, f32[64,32,2]{2,0,1:T(8,128)S(1)} %copy-done.16, f32[64,32,254]{2,0,1:T(8,128)S(1)} %copy-done.10, f32[64,32,1]{2,0,1:T(8,128)S(1)} %copy-done.17, f32[64,32,255]{2,0,1:T(8,128)S(1)} %copy-done.11, ...), kind=kLoop, calls=%fused_computation.57 | loop fusion | flops 152567808 | bytes 31457280 | tf_op jit(solution)/shard_map/stack | solution.py:196
  404.4 2.1 collective-permute-start.4
  406.8 5.2 %collective-permute-done.4 = f32[2,3,32,256]{3,1,2,0:T(4,128)S(1)} collective-permute-done((f32[2,3,32,256]{3,1,2,0:T(4,128)S(1)}, f32[2,3,32,256]{3,1,2,0:T(4,128)S(1)}, u32[]{:S(2)}, u32[]{:S(2)}) %collective-permute-start.4) | collective-permute-done | bytes 196640 | tf_op jit(solution)/shard_map/ppermute | solution.py:21
  412.0 6.3 %collective-permute-done.5 = f32[2,3,32,256]{3,1,2,0:T(4,128)S(1)} collective-permute-done((f32[2,3,32,256]{3,1,2,0:T(4,128)S(1)}, f32[2,3,32,256]{3,1,2,0:T(4,128)S(1)}, u32[]{:S(2)}, u32[]{:S(2)}) %collective-permute-start.5) | collective-permute-done | bytes 196640 | tf_op jit(solution)/shard_map/ppermute | solution.py:19
  419.8 20.3 %fusion.76 = f32[1,64,32,256]{3,1,2,0:T(8,128)S(1)} fusion(f32[1,64,32,256]{3,1,2,0:T(8,128)S(1)} %fusion.21, f32[2,67,32,256]{3,1,2,0:T(8,128)S(1)} %get-tuple-element.21, f32[2,67,32,256]{3,1,2,0:T(8,128)S(1)} %get-tuple-element.20, f32[1,64,32,256]{3,1,2,0:T(8,128)S(1)} %bitcast.178), kind=kLoop, calls=%fused_computation.112 | loop fusion | flops 146276352 | bytes 31457280 | tf_op jit(solution)/shard_map/add | solution.py:129
  440.2 4.8 %collective-permute-start.6 = (f32[2,64,3,256]{3,1,2,0:T(8,128)S(1)}, f32[2,64,3,256]{3,1,2,0:T(8,128)S(1)}, u32[]{:S(2)}, u32[]{:S(2)}) collective-permute-start(f32[2,64,3,256]{3,1,2,0:T(8,128)S(1)} %get-tuple-element.18), channel_id=1, source_target_pairs={{0,1},{1,2},{2,3},{3,4},{4,5},{5,6},{6,7},{7,0},{8,9},{9,10},{10,1... | collective-permute-start | bytes 1179656 | tf_op jit(solution)/shard_map/ppermute | solution.py:19
  445.0 7.7 %collective-permute-done.6 = f32[2,64,3,256]{3,1,2,0:T(8,128)S(1)} collective-permute-done((f32[2,64,3,256]{3,1,2,0:T(8,128)S(1)}, f32[2,64,3,256]{3,1,2,0:T(8,128)S(1)}, u32[]{:S(2)}, u32[]{:S(2)}) %collective-permute-start.6) | collective-permute-done | bytes 393248 | tf_op jit(solution)/shard_map/ppermute | solution.py:19
  452.7 2.7 collective-permute-done.7
  456.4 19.0 %fusion.131 = f32[64,32,256]{2,0,1:T(8,128)S(1)} fusion(f32[64,38,256]{2,0,1:T(8,128)S(1)} %get-tuple-element.17, f32[64,38,256]{2,0,1:T(8,128)S(1)} %get-tuple-element.16), kind=kLoop, calls=%fused_computation.167 | loop fusion | flops 146276352 | bytes 31457280 | tf_op jit(solution)/shard_map/add | solution.py:129
  475.4 2.5 copy.326
  (133 shorter events, 62.6 us)
Async XLA Ops:
  0.0 1.1 copy-start
  56.6 27.0 %all-to-all-start.1 = ((f32[8,1,24576]{2,1,0:T(1,128)}), f32[8,1,24576]{2,1,0:T(1,128)S(1)}, u32[]{:S(2)}, u32[]{:S(2)}) async-start(f32[8,1,24576]{2,1,0:T(1,128)} %reshape.298), calls=%async_computation.1 | async-start | bytes 1572864 | tf_op jit(solution)/shard_map/all_to_all | solution.py:156
  122.4 11.0 %copy-start.2 = (f32[64,32,256]{2,1,0:T(8,128)S(1)}, f32[64,32,256]{2,1,0:T(8,128)}, u32[]{:S(2)}) copy-start(f32[64,32,256]{2,1,0:T(8,128)} %param.3) | copy-start | bytes 6291460
  128.0 25.4 %all-to-all-start.2 = ((f32[8,1,24576]{2,1,0:T(1,128)}), f32[8,1,24576]{2,1,0:T(1,128)}, u32[]{:S(2)}, u32[]{:S(2)}) async-start(f32[8,1,24576]{2,1,0:T(1,128)} %reshape.300), calls=%async_computation.2 | async-start | bytes 1572864 | tf_op jit(solution)/shard_map/all_to_all | solution.py:179
  191.2 14.6 %all-to-all-start.3 = ((f32[4,1,49152]{2,1,0:T(1,128)}), f32[4,1,49152]{2,1,0:T(1,128)}, u32[]{:S(2)}, u32[]{:S(2)}) async-start(f32[4,1,49152]{2,1,0:T(1,128)} %reshape.302), calls=%async_computation.3 | async-start | bytes 1572864 | tf_op jit(solution)/shard_map/all_to_all | solution.py:185
  233.5 3.6 collective-permute-start
  234.3 2.8 collective-permute-start.1
  238.2 69.7 %collective-permute-start.2 = (f32[3,34,1,128]{3,1,0,2:T(8,128)S(1)}, f32[3,34,1,128]{3,1,0,2:T(8,128)S(1)}, u32[]{:S(2)}, u32[]{:S(2)}) collective-permute-start(f32[3,34,1,128]{3,1,0,2:T(8,128)S(1)} %get-tuple-element.60), channel_id=1, source_target_pairs={{0,1},{1,2},{2,3},{3,4},{4,5},{5,6},{6,7},{7,0},{8,9},{9,10},{10,1... | collective-permute-start | bytes 156680 | tf_op jit(solution)/shard_map/ppermute | solution.py:19
  240.0 2.1 copy-start.5
  240.0 68.0 %collective-permute-start.3 = (f32[3,34,1,128]{3,1,0,2:T(8,128)S(1)}, f32[3,34,1,128]{3,1,0,2:T(8,128)S(1)}, u32[]{:S(2)}, u32[]{:S(2)}) collective-permute-start(f32[3,34,1,128]{3,1,0,2:T(8,128)S(1)} %get-tuple-element.61), channel_id=1, source_target_pairs={{1,0},{2,1},{3,2},{4,3},{5,4},{6,5},{7,6},{0,7},{9,8},{10,9},{11,1... | collective-permute-start | bytes 156680 | tf_op jit(solution)/shard_map/ppermute | solution.py:21
  242.0 2.6 copy-start.6
  244.6 2.5 copy-start.8
  247.2 2.5 copy-start.7
  249.7 2.6 copy-start.4
  252.2 2.5 copy-start.3
  254.8 2.5 copy-start.22
  262.1 3.2 copy-start.21
  308.5 1.2 copy-start.23
  371.5 6.2 %copy-start.19 = (f32[64,32,2]{2,0,1:T(8,128)S(1)}, f32[64,32,2]{2,0,1:T(8,128)}, u32[]{:S(2)}) copy-start(f32[64,32,2]{2,0,1:T(8,128)} %copy.350) | copy-start | bytes 49156
  371.5 6.2 %copy-start.20 = (f32[64,32,3]{2,0,1:T(8,128)S(1)}, f32[64,32,3]{2,0,1:T(8,128)}, u32[]{:S(2)}) copy-start(f32[64,32,3]{2,0,1:T(8,128)} %copy.352) | copy-start | bytes 73732
  372.2 5.5 %copy-start.15 = (f32[64,32,3]{2,0,1:T(8,128)S(1)}, f32[64,32,3]{2,0,1:T(8,128)}, u32[]{:S(2)}) copy-start(f32[64,32,3]{2,0,1:T(8,128)} %copy.341) | copy-start | bytes 73732
  372.2 5.5 %copy-start.16 = (f32[64,32,2]{2,0,1:T(8,128)S(1)}, f32[64,32,2]{2,0,1:T(8,128)}, u32[]{:S(2)}) copy-start(f32[64,32,2]{2,0,1:T(8,128)} %copy.343) | copy-start | bytes 49156
  372.2 5.5 %copy-start.17 = (f32[64,32,1]{2,0,1:T(8,128)S(1)}, f32[64,32,1]{2,0,1:T(8,128)}, u32[]{:S(2)}) copy-start(f32[64,32,1]{2,0,1:T(8,128)} %copy.345) | copy-start | bytes 24580
  372.3 5.5 %copy-start.18 = (f32[64,32,1]{2,0,1:T(8,128)S(1)}, f32[64,32,1]{2,0,1:T(8,128)}, u32[]{:S(2)}) copy-start(f32[64,32,1]{2,0,1:T(8,128)} %copy.348) | copy-start | bytes 24580
  374.0 3.7 copy-start.13
  374.0 3.8 copy-start.14
  375.7 3.0 copy-start.11
  375.7 3.6 copy-start.12
  377.4 2.4 copy-start.9
  377.4 3.0 copy-start.10
  404.4 7.5 %collective-permute-start.4 = (f32[2,3,32,256]{3,1,2,0:T(4,128)S(1)}, f32[2,3,32,256]{3,1,2,0:T(4,128)S(1)}, u32[]{:S(2)}, u32[]{:S(2)}) collective-permute-start(f32[2,3,32,256]{3,1,2,0:T(4,128)S(1)} %get-tuple-element.22), channel_id=1, source_target_pairs={{8,0},{16,8},{24,16},{0,24},{9,1},{17,9},{25,17},{1,25},{10,2},{18... | collective-permute-start | bytes 589832 | tf_op jit(solution)/shard_map/ppermute | solution.py:21
  406.5 11.8 %collective-permute-start.5 = (f32[2,3,32,256]{3,1,2,0:T(4,128)S(1)}, f32[2,3,32,256]{3,1,2,0:T(4,128)S(1)}, u32[]{:S(2)}, u32[]{:S(2)}) collective-permute-start(f32[2,3,32,256]{3,1,2,0:T(4,128)S(1)} %get-tuple-element.23), channel_id=1, source_target_pairs={{0,8},{8,16},{16,24},{24,0},{1,9},{9,17},{17,25},{25,1},{2,10},{10... | collective-permute-start | bytes 589832 | tf_op jit(solution)/shard_map/ppermute | solution.py:19
  440.2 12.5 %collective-permute-start.6 = (f32[2,64,3,256]{3,1,2,0:T(8,128)S(1)}, f32[2,64,3,256]{3,1,2,0:T(8,128)S(1)}, u32[]{:S(2)}, u32[]{:S(2)}) collective-permute-start(f32[2,64,3,256]{3,1,2,0:T(8,128)S(1)} %get-tuple-element.18), channel_id=1, source_target_pairs={{0,1},{1,2},{2,3},{3,4},{4,5},{5,6},{6,7},{7,0},{8,9},{9,10},{10,1... | collective-permute-start | bytes 1179656 | tf_op jit(solution)/shard_map/ppermute | solution.py:19
  445.0 10.4 %collective-permute-start.7 = (f32[2,64,3,256]{3,1,2,0:T(8,128)S(1)}, f32[2,64,3,256]{3,1,2,0:T(8,128)S(1)}, u32[]{:S(2)}, u32[]{:S(2)}) collective-permute-start(f32[2,64,3,256]{3,1,2,0:T(8,128)S(1)} %get-tuple-element.19), channel_id=1, source_target_pairs={{1,0},{2,1},{3,2},{4,3},{5,4},{6,5},{7,6},{0,7},{9,8},{10,9},{11,1... | collective-permute-start | bytes 1179656 | tf_op jit(solution)/shard_map/ppermute | solution.py:21
  456.3 21.6 %copy-start.1 = (f32[3,32,16,128]{3,2,1,0:T(8,128)S(1)}, f32[3,32,16,128]{3,2,1,0:T(8,128)}, u32[]{:S(2)}) copy-start(f32[3,32,16,128]{3,2,1,0:T(8,128)} %param.2) | copy-start | bytes 2359300
where the time goes:
time: 483 us; the launch traced here: 478 us
  local copies, waits for them, and re-layouts  199 us (41%)
  other arithmetic  115 us (24%)
  waiting for transfers between devices  62.5 us (13%)
  blocking collectives  54.6 us (11%)
  starting transfers between devices  29.4 us (6%)
  matrix products  16 us (3%)
    unnamed x69, local copies, waits for them, and re-layouts  66.4 us
    pmax x1, blocking collectives, shards(): velocity_peak = lax.pmax(jnp.max(jnp.abs(velocity)), ('row', 'col'))  40.1 us
    add x2, other arithmetic, remesh_rim(): summed = summed + values * kernel_weight(offset - moved)  39.3 us
    another operation x3, other arithmetic, refine_rim(): jnp.stack([lower, upper], axis=grid_axis + 1)  29.5 us
    another operation x1, other arithmetic, shards(): rows_input = jnp.stack([swept, displaced[1]])  23.9 us
    all_to_all x1, waiting for transfers between devices, shards(): lax.all_to_all(spectrum, 'col', split_axis=4, concat_axis=2, tiled=True)  19.6 us
    another operation x3, local copies, waits for them, and re-layouts, rotate(): jnp.stack([real_cos - direction * imag_sin, imag_cos + direction * real_s...  18.6 us
    ppermute x4, waiting for transfers between devices, with_halo(): lax.ppermute(tail, axis, [(i, (i + 1) % count) for i in range(count)])  14.8 us
  transfers between devices with their start and end apart: 11, of which 8 were waited for; matrix products, arithmetic and copies ran while one was open for 8% of the time, Pallas kernels for 0%

commit v1 on v0

--- a/solution.py
+++ b/solution.py
@@ -1,3 +1,4 @@
+import functools
 import math
 import jax
 import jax.numpy as jnp
@@ -7,6 +8,28 @@
 COURANT = 0.9
 EPSILON = 1e-06
 HIGHEST = lax.Precision.HIGHEST
+
+
+def marks_perform(original, named_axis):
+    kept_arr = lax.psum(1, axis_name=named_axis)
+    answer, mid_arr = (kept_arr, lax.axis_index(named_axis))
+    odd = original.shape[4] // answer
+    outer = list(original.shape)
+    outer[4] = odd
+    a_now = outer[2]
+    outer[2] = a_now * answer
+    u_next = jnp.zeros(outer, original.dtype)
+    for p in range(answer):
+        spare = lax.dynamic_slice_in_dim(original, (mid_arr ^ p) * odd, odd, axis=4)
+        if p:
+            spare = lax.ppermute(
+                spare, axis_name=named_axis, perm=[(dd, dd ^ p) for dd in range(answer)]
+            )
+        u_next = lax.dynamic_update_slice_in_dim(u_next, spare, (mid_arr ^ p) * a_now, axis=2)
+    return u_next
+
+
+spread_gates = functools.partial(marks_perform, named_axis="col")
 
 
 def with_halo(cells, sides, width):
@@ -152,13 +175,7 @@
         sin_full,
         -1.0,
     )
-    spectrum = rotate(
-        lax.all_to_all(spectrum, "col", split_axis=4, concat_axis=2, tiled=True),
-        "czkq,zw->ckqw",
-        cos_full,
-        sin_full,
-        -1.0,
-    )
+    spectrum = rotate(spread_gates(spectrum), "czkq,zw->ckqw", cos_full, sin_full, -1.0)
     first_count = spectrum.shape[2]
     second_count = spectrum.shape[3]
     xwaves, xnyquist = wavenumber(lax.axis_index("row") * first_count, first_count, coarse_n)

time: 483 us -> 647 us (1.34)
  local copies, waits for them, and re-layouts: 199 us -> 335 us
  waiting for transfers between devices: 62.5 us -> 95.5 us
  blocking collectives: 54.6 us -> 40.1 us
  starting transfers between devices: 29.4 us -> 37.4 us
    dynamic_update_slice x0 -> x8, local copies, waits for them, and re-layouts: none -> 162 us  [marks_perform(): lax.dynamic_update_slice_in_dim(u_next, spare, (mid_arr ^ p) * a_now, axi...]
    ppermute x0 -> x7, waiting for transfers between devices: none -> 42.8 us  [marks_perform(): lax.ppermute(spare, axis_name=named_axis, perm=[(dd, dd ^ p) for dd in ra...]
    all_to_all x1 -> x0, blocking collectives: 14.5 us -> none  [shards(): lax.all_to_all(forward, 'row', split_axis=4, concat_axis=2, tiled=True)]
    ppermute x0 -> x7, starting transfers between devices: none -> 11.5 us  [marks_perform(): lax.ppermute(spare, axis_name=named_axis, perm=[(dd, dd ^ p) for dd in ra...]
    all_to_all x1, waiting for transfers between devices: 19.6 us -> 9.71 us  [shards(): lax.all_to_all(forward, 'row', split_axis=4, concat_axis=2, tiled=True)]
    unnamed x69 -> x71, local copies, waits for them, and re-layouts: 66.4 us -> 57.2 us
    ppermute x0 -> x7, local copies, waits for them, and re-layouts: none -> 9.08 us  [marks_perform(): lax.ppermute(spare, axis_name=named_axis, perm=[(dd, dd ^ p) for dd in ra...]
    all_to_all x1 -> x0, local copies, waits for them, and re-layouts: 8.02 us -> none  [shards(): lax.all_to_all(spectrum, 'col', split_axis=4, concat_axis=2, tiled=True)]
  transfers between devices with their start and end apart: 11 -> 18, of which waited for: 8 -> 9; matrix products, arithmetic and copies ran while one was open for 8% -> 29% of each run, Pallas kernels for 0% -> 0%
where the time goes in v1:
time: 647 us; the launch traced here: 643 us
  local copies, waits for them, and re-layouts  335 us (52%)
  other arithmetic  117 us (18%)
  waiting for transfers between devices  95.5 us (15%)
  blocking collectives  40.1 us (6%)
  starting transfers between devices  37.4 us (6%)
  matrix products  16 us (2%)
    dynamic_update_slice x8, local copies, waits for them, and re-layouts, marks_perform(): lax.dynamic_update_slice_in_dim(u_next, spare, (mid_arr ^ p) * a_now, axi...  162 us
    unnamed x71, local copies, waits for them, and re-layouts  57.2 us
    ppermute x7, waiting for transfers between devices, marks_perform(): lax.ppermute(spare, axis_name=named_axis, perm=[(dd, dd ^ p) for dd in ra...  42.8 us
    pmax x1, blocking collectives, shards(): velocity_peak = lax.pmax(jnp.max(jnp.abs(velocity)), ('row', 'col'))  40.1 us
    add x2, other arithmetic, remesh_rim(): summed = summed + values * kernel_weight(offset - moved)  39.3 us
    another operation x3, other arithmetic, refine_rim(): jnp.stack([lower, upper], axis=grid_axis + 1)  29.2 us
    another operation x1, other arithmetic, shards(): rows_input = jnp.stack([swept, displaced[1]])  24 us
    ppermute x4, waiting for transfers between devices, with_halo(): lax.ppermute(tail, axis, [(i, (i + 1) % count) for i in range(count)])  14.8 us
  transfers between devices with their start and end apart: 18, of which 9 were waited for; matrix products, arithmetic and copies ran while one was open for 29% of the time, Pallas kernels for 0%

profile of v1, /device:TPU:1, one launch (start us, length us, event | category | flops | bytes accessed | tf_op | source)
XLA Modules:
  0.0 642.6 jit_solution(1982547323373641452)
XLA Ops:
  3.2 2.6 copy.328
  5.7 4.4 reshape.292
  10.1 4.5 all-to-all-start
  15.0 9.7 %all-to-all-done = f32[4,1,49152]{2,1,0:T(1,128)S(1)} async-done(((f32[4,1,49152]{2,1,0:T(1,128)}), f32[4,1,49152]{2,1,0:T(1,128)S(1)}, u32[]{:S(2)}, u32[]{:S(2)}) %all-to-all-start) | async-done | bytes 786464 | tf_op jit(solution)/shard_map/all_to_all | solution.py:172
  25.3 3.0 reduce
  28.3 2.7 reshape.293
  31.0 3.7 copy.329
  45.8 3.2 fusion.202
  52.1 2.4 collective-permute-start.3
  56.5 3.4 collective-permute-start.5
  59.8 42.7 %collective-permute-done.1 = f32[2,3,16,16,16]{4,3,2,1,0:T(8,128)S(1)} collective-permute-done((f32[2,3,16,16,16]{4,3,2,1,0:T(8,128)S(1)}, f32[2,3,16,16,16]{4,3,2,1,0:T(8,128)S(1)}, u32[]{:S(2)}, u32[]{:S(2)}) %collective-permute-start.1) | collective-permute-done | bytes 98336 | tf_op jit(solution)/shard_map/ppermute | solution.py:25
  102.6 2.3 collective-permute-start.6
  105.3 21.8 %dynamic_update_slice.24 = f32[2,3,128,16,16]{2,4,3,1,0:T(8,128)S(1)} dynamic-update-slice(f32[2,3,128,16,16]{2,4,3,1,0:T(8,128)S(1)} %broadcast_in_dim.53, f32[2,3,16,16,16]{2,4,3,1,0:T(8,128)S(1)} %copy.332, s32[]{:T(128)} %constant.301.clone.1, s32[]{:T(128)} %constant.301.clone.1, s32[]{:T(128)S(6)} %select_n.350, s32[]{:T(128)} %constant.301.clone.1, s32[]{:T(128)} %constant.301.clone.1) | dynamic-update-slice | bytes 196612 | tf_op jit(solution)/shard_map/dynamic_update_slice | solution.py:28
  128.6 9.3 %dynamic_update_slice.25 = f32[2,3,128,16,16]{2,4,3,1,0:T(8,128)S(1)} dynamic-update-slice(f32[2,3,128,16,16]{2,4,3,1,0:T(8,128)S(1)} %dynamic_update_slice.24, f32[2,3,16,16,16]{2,4,3,1,0:T(8,128)S(1)} %copy.333, s32[]{:T(128)} %constant.301.clone.1, s32[]{:T(128)} %constant.301.clone.1, s32[]{:T(128)S(6)} %select_n.351, s32[]{:T(128)} %constant.301.clone.1, s32[]{:T(128)} %constant.301.clone.1) | dynamic-update-slice | bytes 196612 | tf_op jit(solution)/shard_map/dynamic_update_slice | solution.py:28
  138.3 21.8 %dynamic_update_slice.26 = f32[2,3,128,16,16]{2,4,3,1,0:T(8,128)S(1)} dynamic-update-slice(f32[2,3,128,16,16]{2,4,3,1,0:T(8,128)S(1)} %dynamic_update_slice.25, f32[2,3,16,16,16]{2,4,3,1,0:T(8,128)S(1)} %copy.334, s32[]{:T(128)} %constant.301.clone.1, s32[]{:T(128)} %constant.301.clone.1, s32[]{:T(128)S(6)} %select_n.352, s32[]{:T(128)} %constant.301.clone.1, s32[]{:T(128)} %constant.301.clone.1) | dynamic-update-slice | bytes 196612 | tf_op jit(solution)/shard_map/dynamic_update_slice | solution.py:28
  161.5 21.8 %dynamic_update_slice.27 = f32[2,3,128,16,16]{2,4,3,1,0:T(8,128)S(1)} dynamic-update-slice(f32[2,3,128,16,16]{2,4,3,1,0:T(8,128)S(1)} %dynamic_update_slice.26, f32[2,3,16,16,16]{2,4,3,1,0:T(8,128)S(1)} %copy.335, s32[]{:T(128)} %constant.301.clone.1, s32[]{:T(128)} %constant.301.clone.1, s32[]{:T(128)S(6)} %select_n.353, s32[]{:T(128)} %constant.301.clone.1, s32[]{:T(128)} %constant.301.clone.1) | dynamic-update-slice | bytes 196612 | tf_op jit(solution)/shard_map/dynamic_update_slice | solution.py:28
  184.8 21.8 %dynamic_update_slice.28 = f32[2,3,128,16,16]{2,4,3,1,0:T(8,128)S(1)} dynamic-update-slice(f32[2,3,128,16,16]{2,4,3,1,0:T(8,128)S(1)} %dynamic_update_slice.27, f32[2,3,16,16,16]{2,4,3,1,0:T(8,128)S(1)} %copy.336, s32[]{:T(128)} %constant.301.clone.1, s32[]{:T(128)} %constant.301.clone.1, s32[]{:T(128)S(6)} %select_n.354, s32[]{:T(128)} %constant.301.clone.1, s32[]{:T(128)} %constant.301.clone.1) | dynamic-update-slice | bytes 196612 | tf_op jit(solution)/shard_map/dynamic_update_slice | solution.py:28
  208.0 21.8 %dynamic_update_slice.29 = f32[2,3,128,16,16]{2,4,3,1,0:T(8,128)S(1)} dynamic-update-slice(f32[2,3,128,16,16]{2,4,3,1,0:T(8,128)S(1)} %dynamic_update_slice.28, f32[2,3,16,16,16]{2,4,3,1,0:T(8,128)S(1)} %copy.337, s32[]{:T(128)} %constant.301.clone.1, s32[]{:T(128)} %constant.301.clone.1, s32[]{:T(128)S(6)} %select_n.355, s32[]{:T(128)} %constant.301.clone.1, s32[]{:T(128)} %constant.301.clone.1) | dynamic-update-slice | bytes 196612 | tf_op jit(solution)/shard_map/dynamic_update_slice | solution.py:28
  231.3 21.8 %dynamic_update_slice.30 = f32[2,3,128,16,16]{2,4,3,1,0:T(8,128)S(1)} dynamic-update-slice(f32[2,3,128,16,16]{2,4,3,1,0:T(8,128)S(1)} %dynamic_update_slice.29, f32[2,3,16,16,16]{2,4,3,1,0:T(8,128)S(1)} %copy.338, s32[]{:T(128)} %constant.301.clone.1, s32[]{:T(128)} %constant.301.clone.1, s32[]{:T(128)S(6)} %select_n.356, s32[]{:T(128)} %constant.301.clone.1, s32[]{:T(128)} %constant.301.clone.1) | dynamic-update-slice | bytes 196612 | tf_op jit(solution)/shard_map/dynamic_update_slice | solution.py:28
  254.5 22.0 %dynamic_update_slice.31 = f32[2,3,128,16,16]{2,4,3,1,0:T(8,128)S(1)} dynamic-update-slice(f32[2,3,128,16,16]{2,4,3,1,0:T(8,128)S(1)} %dynamic_update_slice.30, f32[2,3,16,16,16]{2,4,3,1,0:T(8,128)S(1)} %copy.339, s32[]{:T(128)} %constant.301.clone.1, s32[]{:T(128)} %constant.301.clone.1, s32[]{:T(128)S(6)} %select_n.357, s32[]{:T(128)} %constant.301.clone.1, s32[]{:T(128)} %constant.301.clone.1) | dynamic-update-slice | bytes 196612 | tf_op jit(solution)/shard_map/dynamic_update_slice | solution.py:28
  282.5 5.9 copy.340
  288.4 5.6 reshape.294
  294.1 4.4 all-to-all-start.1
  298.5 2.8 fusion.359
  301.2 2.7 fusion.361
  304.0 14.4 %all-to-all-done.1 = f32[8,1,24576]{2,1,0:T(1,128)} async-done(((f32[8,1,24576]{2,1,0:T(1,128)}), f32[8,1,24576]{2,1,0:T(1,128)}, u32[]{:S(2)}, u32[]{:S(2)}) %all-to-all-start.1) | async-done | bytes 786464 | tf_op jit(solution)/shard_map/all_to_all | solution.py:196
  318.4 3.7 reduce.1
  322.1 4.7 reshape.295
  326.8 6.4 copy.395
  333.2 3.1 fusion.349
  336.3 2.4 squeeze.26
  339.4 2.9 squeeze.27
  344.6 5.9 copy.342
  350.5 5.5 reshape.296
  355.9 4.2 all-to-all-start.2
  361.8 2.7 fusion.363
  364.5 6.0 all-to-all-done.2
  370.5 3.9 reduce.2
  374.4 4.8 reshape.297
  379.3 6.7 %copy.343 = f32[2,3,16,16,4,32]{5,3,2,4,1,0:T(8,128)} copy(f32[2,3,16,16,4,32]{3,2,1,0,5,4:T(8,128)} %bitcast.175) | data formatting | bytes 1572864 | tf_op jit(solution)/shard_map/all_to_all | solution.py:202
  385.9 3.8 fusion.350
  389.8 2.8 copy.345
  406.8 2.5 copy.384
  409.3 2.5 copy.386
  411.9 2.5 copy.388
  414.4 2.6 copy.389
  417.0 2.5 copy.391
  419.5 2.5 copy.393
  431.9 40.1 %pmax.7 = f32[]{:T(128)} all-reduce(f32[]{:T(128)} %get-tuple-element.5), channel_id=1, replica_groups=mesh['row'=4,'col'=8] {'row','col'}, use_global_device_ids=true, to_apply=%region_1.2 | all-reduce | flops 1 | bytes 8 | tf_op jit(solution)/shard_map/pmax | solution.py:206
  476.8 9.8 %copy.352 = f32[3,34,18,128,2]{1,4,3,2,0:T(2,128)} copy(f32[3,34,18,128,2]{3,1,2,0,4:T(8,128)} %pad_maximum_fusion.3) | data formatting | bytes 3760128 | tf_op jit(solution)/shard_map/stack | solution.py:122
  486.6 11.8 %fusion.3 = (f32[3,32,1,18,256]{1,4,3,0,2:T(8,128)}, f32[3,32,1,18,256]{1,4,3,0,2:T(8,128)}) fusion(f32[3,34,18,256]{1,3,2,0:T(8,128)} %bitcast.167), kind=kLoop, calls=%fused_computation.6 | loop fusion | flops 2211840 | bytes 8847360 | tf_op jit(solution)/shard_map/stack | solution.py:132
  498.4 12.6 %pad_maximum_fusion = f32[3,32,2,18,256]{1,4,3,0,2:T(8,128)} fusion(f32[3,32,1,18,256]{1,4,3,0,2:T(8,128)} %get-tuple-element.8, f32[3,32,1,18,256]{1,4,3,0,2:T(8,128)} %get-tuple-element.7), kind=kLoop, calls=%fused_computation | loop fusion | flops 884736 | bytes 7077888 | tf_op jit(solution)/shard_map/stack | solution.py:132
  511.0 10.9 %copy.353 = f32[3,32,2,18,256]{4,2,1,3,0:T(2,128)} copy(f32[3,32,2,18,256]{1,4,3,0,2:T(8,128)} %pad_maximum_fusion) | data formatting | bytes 7077888 | tf_op jit(solution)/shard_map/stack | solution.py:132
  521.9 5.8 reshape.283
  527.7 4.8 fusion.7
  544.9 24.0 %fusion.21 = f32[1,64,32,256]{3,1,2,0:T(8,128)S(1)} fusion(f32[64,32,3]{2,0,1:T(8,128)S(1)} %copy-done.15, f32[64,32,253]{2,0,1:T(8,128)S(1)} %copy-done.9, f32[64,32,2]{2,0,1:T(8,128)S(1)} %copy-done.16, f32[64,32,254]{2,0,1:T(8,128)S(1)} %copy-done.10, f32[64,32,1]{2,0,1:T(8,128)S(1)} %copy-done.17, f32[64,32,255]{2,0,1:T(8,128)S(1)} %copy-done.11, ...), kind=kLoop, calls=%fused_computation.57 | loop fusion | flops 152567808 | bytes 31457280 | tf_op jit(solution)/shard_map/stack | solution.py:213
  571.4 5.2 collective-permute-done.11
  576.6 6.3 collective-permute-done.12
  584.4 20.3 %fusion.76 = f32[1,64,32,256]{3,1,2,0:T(8,128)S(1)} fusion(f32[1,64,32,256]{3,1,2,0:T(8,128)S(1)} %fusion.21, f32[2,67,32,256]{3,1,2,0:T(8,128)S(1)} %get-tuple-element.19, f32[2,67,32,256]{3,1,2,0:T(8,128)S(1)} %get-tuple-element.18, f32[1,64,32,256]{3,1,2,0:T(8,128)S(1)} %bitcast.170), kind=kLoop, calls=%fused_computation.112 | loop fusion | flops 146276352 | bytes 31457280 | tf_op jit(solution)/shard_map/add | solution.py:152
  604.8 4.8 collective-permute-start.13
  609.6 7.7 %collective-permute-done.13 = f32[2,64,3,256]{3,1,2,0:T(8,128)S(1)} collective-permute-done((f32[2,64,3,256]{3,1,2,0:T(8,128)S(1)}, f32[2,64,3,256]{3,1,2,0:T(8,128)S(1)}, u32[]{:S(2)}, u32[]{:S(2)}) %collective-permute-start.13) | collective-permute-done | bytes 393248 | tf_op jit(solution)/shard_map/ppermute | solution.py:42
  617.3 2.7 collective-permute-done.14
  620.9 19.0 %fusion.131 = f32[64,32,256]{2,0,1:T(8,128)S(1)} fusion(f32[64,38,256]{2,0,1:T(8,128)S(1)} %get-tuple-element.15, f32[64,38,256]{2,0,1:T(8,128)S(1)} %get-tuple-element.14), kind=kLoop, calls=%fused_computation.167 | loop fusion | flops 146276352 | bytes 31457280 | tf_op jit(solution)/shard_map/add | solution.py:152
  639.9 2.5 copy.368
  (160 shorter events, 85.5 us)
Async XLA Ops:
  0.0 1.1 copy-start
  10.1 14.6 %all-to-all-start = ((f32[4,1,49152]{2,1,0:T(1,128)}), f32[4,1,49152]{2,1,0:T(1,128)S(1)}, u32[]{:S(2)}, u32[]{:S(2)}) async-start(f32[4,1,49152]{2,1,0:T(1,128)} %reshape.292), calls=%async_computation | async-start | bytes 1572864 | tf_op jit(solution)/shard_map/all_to_all | solution.py:172
  49.0 7.5 %collective-permute-start = (f32[2,3,16,16,16]{4,3,2,1,0:T(8,128)S(1)}, f32[2,3,16,16,16]{4,3,2,1,0:T(8,128)S(1)}, u32[]{:S(2)}, u32[]{:S(2)}) collective-permute-start(f32[2,3,16,16,16]{4,3,2,1,0:T(8,128)S(1)} %get-tuple-element.66), channel_id=1, source_target_pairs={{0,1},{1,0},{2,3},{3,2},{4,5},{5,4},{6,7},{7,6},{8,9},{9,8},{10,11... | collective-permute-start | bytes 294920 | tf_op jit(solution)/shard_map/ppermute | solution.py:25
  50.4 52.1 %collective-permute-start.1 = (f32[2,3,16,16,16]{4,3,2,1,0:T(8,128)S(1)}, f32[2,3,16,16,16]{4,3,2,1,0:T(8,128)S(1)}, u32[]{:S(2)}, u32[]{:S(2)}) collective-permute-start(f32[2,3,16,16,16]{4,3,2,1,0:T(8,128)S(1)} %get-tuple-element.67), channel_id=1, source_target_pairs={{0,2},{1,3},{2,0},{3,1},{4,6},{5,7},{6,4},{7,5},{8,10},{9,11},{10,... | collective-permute-start | bytes 294920 | tf_op jit(solution)/shard_map/ppermute | solution.py:25
  51.8 108.3 %collective-permute-start.2 = (f32[2,3,16,16,16]{4,3,2,1,0:T(8,128)}, f32[2,3,16,16,16]{4,3,2,1,0:T(8,128)}, u32[]{:S(2)}, u32[]{:S(2)}) collective-permute-start(f32[2,3,16,16,16]{4,3,2,1,0:T(8,128)} %get-tuple-element.68), channel_id=1, source_target_pairs={{0,3},{1,2},{2,1},{3,0},{4,7},{5,6},{6,5},{7,4},{8,11},{9,10},{10,... | collective-permute-start | bytes 294920 | tf_op jit(solution)/shard_map/ppermute | solution.py:25
  52.1 131.2 %collective-permute-start.3 = (f32[2,3,16,16,16]{4,3,2,1,0:T(8,128)}, f32[2,3,16,16,16]{4,3,2,1,0:T(8,128)}, u32[]{:S(2)}, u32[]{:S(2)}) collective-permute-start(f32[2,3,16,16,16]{4,3,2,1,0:T(8,128)} %get-tuple-element.69), channel_id=1, source_target_pairs={{0,4},{1,5},{2,6},{3,7},{4,0},{5,1},{6,2},{7,3},{8,12},{9,13},{10,... | collective-permute-start | bytes 294920 | tf_op jit(solution)/shard_map/ppermute | solution.py:25
  56.1 150.5 %collective-permute-start.4 = (f32[2,3,16,16,16]{4,3,2,1,0:T(8,128)}, f32[2,3,16,16,16]{4,3,2,1,0:T(8,128)}, u32[]{:S(2)}, u32[]{:S(2)}) collective-permute-start(f32[2,3,16,16,16]{4,3,2,1,0:T(8,128)} %get-tuple-element.71), channel_id=1, source_target_pairs={{0,5},{1,4},{2,7},{3,6},{4,1},{5,0},{6,3},{7,2},{8,13},{9,12},{10,... | collective-permute-start | bytes 294920 | tf_op jit(solution)/shard_map/ppermute | solution.py:25
  56.5 48.4 %copy-start.25 = (f32[2,3,16,16,16]{4,3,2,1,0:T(8,128)}, f32[2,3,16,16,16]{4,3,2,1,0:T(8,128)S(1)}, u32[]{:S(2)}) copy-start(f32[2,3,16,16,16]{4,3,2,1,0:T(8,128)S(1)} %collective-permute-done) | copy-start | bytes 294916
  56.5 173.3 %collective-permute-start.5 = (f32[2,3,16,16,16]{4,3,2,1,0:T(8,128)}, f32[2,3,16,16,16]{4,3,2,1,0:T(8,128)}, u32[]{:S(2)}, u32[]{:S(2)}) collective-permute-start(f32[2,3,16,16,16]{4,3,2,1,0:T(8,128)} %get-tuple-element.70), channel_id=1, source_target_pairs={{0,6},{1,7},{2,4},{3,5},{4,2},{5,3},{6,0},{7,1},{8,14},{9,15},{10,... | collective-permute-start | bytes 294920 | tf_op jit(solution)/shard_map/ppermute | solution.py:25
  102.6 2.3 copy-start.23
  102.6 150.5 %collective-permute-start.6 = (f32[2,3,16,16,16]{4,3,2,1,0:T(8,128)}, f32[2,3,16,16,16]{4,3,2,1,0:T(8,128)}, u32[]{:S(2)}, u32[]{:S(2)}) collective-permute-start(f32[2,3,16,16,16]{4,3,2,1,0:T(8,128)} %get-tuple-element.64), channel_id=1, source_target_pairs={{0,7},{1,6},{2,5},{3,4},{4,3},{5,2},{6,1},{7,0},{8,15},{9,14},{10,... | collective-permute-start | bytes 294920 | tf_op jit(solution)/shard_map/ppermute | solution.py:25
  105.3 32.6 %copy-start.24 = (f32[2,3,16,16,16]{4,3,2,1,0:T(8,128)S(1)}, f32[2,3,16,16,16]{4,3,2,1,0:T(8,128)}, u32[]{:S(2)}) copy-start(f32[2,3,16,16,16]{4,3,2,1,0:T(8,128)} %copy-done.23) | copy-start | bytes 294916
  288.4 10.0 %copy-start.2 = (f32[64,32,256]{2,1,0:T(8,128)S(1)}, f32[64,32,256]{2,1,0:T(8,128)}, u32[]{:S(2)}) copy-start(f32[64,32,256]{2,1,0:T(8,128)} %param.3) | copy-start | bytes 6291460
  294.1 24.3 %all-to-all-start.1 = ((f32[8,1,24576]{2,1,0:T(1,128)}), f32[8,1,24576]{2,1,0:T(1,128)}, u32[]{:S(2)}, u32[]{:S(2)}) async-start(f32[8,1,24576]{2,1,0:T(1,128)} %reshape.294), calls=%async_computation.1 | async-start | bytes 1572864 | tf_op jit(solution)/shard_map/all_to_all | solution.py:196
  355.9 14.6 %all-to-all-start.2 = ((f32[4,1,49152]{2,1,0:T(1,128)}), f32[4,1,49152]{2,1,0:T(1,128)}, u32[]{:S(2)}, u32[]{:S(2)}) async-start(f32[4,1,49152]{2,1,0:T(1,128)} %reshape.296), calls=%async_computation.2 | async-start | bytes 1572864 | tf_op jit(solution)/shard_map/all_to_all | solution.py:202
  398.2 3.6 collective-permute-start.7
  399.0 2.8 collective-permute-start.8
  403.0 69.8 %collective-permute-start.9 = (f32[3,34,1,128]{3,1,0,2:T(8,128)S(1)}, f32[3,34,1,128]{3,1,0,2:T(8,128)S(1)}, u32[]{:S(2)}, u32[]{:S(2)}) collective-permute-start(f32[3,34,1,128]{3,1,0,2:T(8,128)S(1)} %get-tuple-element.58), channel_id=1, source_target_pairs={{0,1},{1,2},{2,3},{3,4},{4,5},{5,6},{6,7},{7,0},{8,9},{9,10},{10,1... | collective-permute-start | bytes 156680 | tf_op jit(solution)/shard_map/ppermute | solution.py:42
  404.8 1.9 copy-start.5
  404.8 68.0 %collective-permute-start.10 = (f32[3,34,1,128]{3,1,0,2:T(8,128)S(1)}, f32[3,34,1,128]{3,1,0,2:T(8,128)S(1)}, u32[]{:S(2)}, u32[]{:S(2)}) collective-permute-start(f32[3,34,1,128]{3,1,0,2:T(8,128)S(1)} %get-tuple-element.59), channel_id=1, source_target_pairs={{1,0},{2,1},{3,2},{4,3},{5,4},{6,5},{7,6},{0,7},{9,8},{10,9},{11,1... | collective-permute-start | bytes 156680 | tf_op jit(solution)/shard_map/ppermute | solution.py:44
  406.8 2.6 copy-start.6
  409.3 2.5 copy-start.8
  411.9 2.5 copy-start.7
  414.4 2.6 copy-start.4
  417.0 2.5 copy-start.3
  419.5 2.5 copy-start.21
  426.9 3.2 copy-start.20
  473.3 1.2 copy-start.22
  535.9 6.2 copy-start.19
  536.6 5.4 copy-start.15
  536.7 5.4 copy-start.16
  536.7 5.4 copy-start.17
  536.7 5.4 copy-start.18
  538.4 3.7 copy-start.13
  538.4 3.8 copy-start.14
  540.1 3.0 copy-start.11
  540.1 3.6 copy-start.12
  541.8 2.5 copy-start.9
  541.8 3.1 copy-start.10
  569.0 7.6 %collective-permute-start.11 = (f32[2,3,32,256]{3,1,2,0:T(4,128)S(1)}, f32[2,3,32,256]{3,1,2,0:T(4,128)S(1)}, u32[]{:S(2)}, u32[]{:S(2)}) collective-permute-start(f32[2,3,32,256]{3,1,2,0:T(4,128)S(1)} %get-tuple-element.20), channel_id=1, source_target_pairs={{8,0},{16,8},{24,16},{0,24},{9,1},{17,9},{25,17},{1,25},{10,2},{18... | collective-permute-start | bytes 589832 | tf_op jit(solution)/shard_map/ppermute | solution.py:44
  571.1 11.8 %collective-permute-start.12 = (f32[2,3,32,256]{3,1,2,0:T(4,128)S(1)}, f32[2,3,32,256]{3,1,2,0:T(4,128)S(1)}, u32[]{:S(2)}, u32[]{:S(2)}) collective-permute-start(f32[2,3,32,256]{3,1,2,0:T(4,128)S(1)} %get-tuple-element.21), channel_id=1, source_target_pairs={{0,8},{8,16},{16,24},{24,0},{1,9},{9,17},{17,25},{25,1},{2,10},{10... | collective-permute-start | bytes 589832 | tf_op jit(solution)/shard_map/ppermute | solution.py:42
  604.8 12.5 %collective-permute-start.13 = (f32[2,64,3,256]{3,1,2,0:T(8,128)S(1)}, f32[2,64,3,256]{3,1,2,0:T(8,128)S(1)}, u32[]{:S(2)}, u32[]{:S(2)}) collective-permute-start(f32[2,64,3,256]{3,1,2,0:T(8,128)S(1)} %get-tuple-element.16), channel_id=1, source_target_pairs={{0,1},{1,2},{2,3},{3,4},{4,5},{5,6},{6,7},{7,0},{8,9},{9,10},{10,1... | collective-permute-start | bytes 1179656 | tf_op jit(solution)/shard_map/ppermute | solution.py:42
  609.6 10.4 %collective-permute-start.14 = (f32[2,64,3,256]{3,1,2,0:T(8,128)S(1)}, f32[2,64,3,256]{3,1,2,0:T(8,128)S(1)}, u32[]{:S(2)}, u32[]{:S(2)}) collective-permute-start(f32[2,64,3,256]{3,1,2,0:T(8,128)S(1)} %get-tuple-element.17), channel_id=1, source_target_pairs={{1,0},{2,1},{3,2},{4,3},{5,4},{6,5},{7,6},{0,7},{9,8},{10,9},{11,1... | collective-permute-start | bytes 1179656 | tf_op jit(solution)/shard_map/ppermute | solution.py:44
  620.9 21.6 %copy-start.1 = (f32[3,32,16,128]{3,2,1,0:T(8,128)S(1)}, f32[3,32,16,128]{3,2,1,0:T(8,128)}, u32[]{:S(2)}) copy-start(f32[3,32,16,128]{3,2,1,0:T(8,128)} %param.2) | copy-start | bytes 2359300
